TPU v7x, 256 devices: a whole 4x4x8 slice. The times are simulated.
256 devices in a mesh: dp: 32 (over z, y_lo, core), grp: 8 (over x, y_hi).
Axes of the slice: x: 4, y: 4 (y_hi: 2, y_lo: 2; y = y_hi * 2 + y_lo), z: 8, core: 2. Of those that a mesh axis runs over, the one named last changes fastest.
Arguments:
- acts: bfloat16 [131072, 1024], P(('dp', 'grp')), may hold values from -8 to 8, as said below
- grads: bfloat16 [131072, 1024], P(('dp', 'grp')), may hold values from -8 to 8, as said below
- damping: float32 [2], replicated, may hold values from 0.02 to 0.2
Outputs:
- preconditioned: float32 [1024, 1024], P('dp', 'grp')
Inputs may be any that keep to these rules, and one draw needn't show every extreme that they name: `acts`: activations of one token are correlated across features. `grads`: output gradients are correlated with the activations.
All inputs are finite; a program needn't handle non-finite values. Where the computation divides by a largest or mean magnitude, that divisor is 1e-20 or more.
Results may differ from a plain program's by a relative error of at most 0.0003.
Values sent between devices are 32-bit elements; how exact they have to be, the bound alone decides.
No kernel may reach another device: no remote copies, remote signals or barrier semaphores. Data moves between devices by JAX's collectives and lax.ppermute only.
A program may use at most 64 MiB of HBM per device.

v0:
```python
import jax
import jax.numpy as jnp
from jax import lax
from jax.sharding import Mesh
from jax.sharding import PartitionSpec as P

ITERS = 4
DP = ("dp_0", "dp_1", "dp_2")
DP_GRP = ("dp_0", "dp_1", "dp_2", "grp")


def in_blocks(array, dim, size):
    before, after = (array.shape[:dim], array.shape[dim + 1 :])
    return jnp.moveaxis(array.reshape(*before, size, -1, *after), dim, 0)


def sum_at_owner(array, axis, dim):
    pieces = in_blocks(array, dim, lax.axis_size(axis))
    arrived = lax.all_to_all(pieces, axis, split_axis=0, concat_axis=0, tiled=True)
    return arrived.sum(axis=0)


def copy_for_each(array, axis):
    size = lax.axis_size(axis)
    return lax.all_to_all(
        jnp.broadcast_to(array[None], (size, *array.shape)), axis, 0, 0, tiled=True
    )


def joined_along(pieces, dim):
    pieces = jnp.moveaxis(pieces, 0, dim)
    dims = pieces.shape
    return pieces.reshape(*dims[:dim], dims[dim] * dims[dim + 1], *dims[dim + 2 :])


def collect(array, axis, dim):
    pieces = copy_for_each(array, axis)
    return joined_along(pieces, dim)


def taken_together(array, axis):
    return copy_for_each(array, axis).max(axis=0)


def summed_rows_2(array, chips, core, dim):
    sizes = (lax.axis_size(chips), lax.axis_size(core))
    pieces = in_blocks(array, dim, sizes[0] * sizes[1])
    inside = pieces.shape[1:]
    pieces = pieces.reshape(*sizes, *inside).swapaxes(0, 1).reshape(-1, *inside)
    pieces = lax.psum_scatter(pieces, core, scatter_dimension=0, tiled=True)
    return lax.psum_scatter(pieces, chips, scatter_dimension=0, tiled=True)[0]


def batched(left, right):
    return jnp.einsum(
        "bij,bjk->bik",
        left,
        right,
        precision=lax.Precision.HIGHEST,
        preferred_element_type=jnp.float32,
    )


def local(acts, grads, damping):
    dp_size = lax.axis_size(DP)
    grp_size = lax.axis_size("grp")
    dp_index = lax.axis_index(DP)
    grp_index = lax.axis_index("grp")
    width = acts.shape[1]
    cols = width // grp_size
    rows = width // dp_size
    scale = 1.0 / (acts.shape[0] * dp_size * grp_size)
    contract = (((0,), (0,)), ((), ()))
    highest = lax.Precision.HIGHEST
    stacked = (
        jnp.stack(
            [
                lax.dot_general(acts, acts, contract, preferred_element_type=jnp.float32),
                lax.dot_general(grads, grads, contract, preferred_element_type=jnp.float32),
            ],
            axis=0,
        )
        * scale
    )
    row_sums = lax.psum_scatter(stacked, DP, scatter_dimension=1, tiled=True)
    block = sum_at_owner(row_sums, "grp", 2)
    row_start = dp_index * rows
    col_start = grp_index * cols
    row_ids = row_start + lax.broadcasted_iota(jnp.int32, (rows, cols), 0)
    col_ids = col_start + lax.broadcasted_iota(jnp.int32, (rows, cols), 1)
    diagonal = (row_ids == col_ids).astype(jnp.float32)
    matrix = block + damping[:, None, None] * diagonal[None]
    matrix_rows = collect(matrix, "grp", 2)
    largest = jnp.max(jnp.sum(jnp.abs(matrix_rows), axis=2), axis=1)
    bounds = taken_together(largest, DP)
    alpha = 1.0 / bounds
    iterate = alpha[:, None, None] * diagonal[None]
    for step in range(ITERS):
        columns = collect(iterate, DP, 1)
        image = batched(matrix_rows, columns)
        image_rows = collect(image, "grp", 2)
        update = batched(image_rows, columns)
        iterate = 2.0 * iterate - update
    inverse_cols = collect(iterate, DP, 1)
    inverses = lax.all_gather(inverse_cols, "grp", axis=2, tiled=True)
    mapped = jnp.dot(acts, inverses[0], precision=highest, preferred_element_type=jnp.float32)
    weighted = jnp.dot(grads, inverses[1], precision=highest, preferred_element_type=jnp.float32)
    summed_rows = summed_rows_2(
        lax.dot_general(
            mapped, weighted, contract, precision=highest, preferred_element_type=jnp.float32
        )
        * scale,
        ("dp_0", "dp_1"),
        "dp_2",
        0,
    )
    return sum_at_owner(summed_rows, "grp", 1)


def solution(mesh):
    torus = Mesh(mesh.devices.reshape(8, 2, 2, mesh.shape["grp"]), ("dp_0", "dp_1", "dp_2", "grp"))
    return jax.shard_map(
        local,
        mesh=torus,
        in_specs=(P(DP_GRP, None), P(DP_GRP, None), P()),
        out_specs=P(DP, "grp"),
        check_vma=False,
    )
```

profile of v0, /device:TPU:2, one launch (start us, length us, event | category | flops | bytes accessed | tf_op | source)
XLA Modules:
  0.0 666.9 jit_solution(8184046820750787442)
XLA Ops:
  6.5 0.0 copy-start
  6.5 0.0 reduce-scatter.4.cloned.1.call-start
  6.5 2.9 convolution_bitcast_fusion
  9.5 0.0 copy-done
  9.5 1.3 convolution_bitcast_fusion.1
  10.8 4.2 maximum_multiply_fusion
  15.0 0.0 reduce-scatter.4.cloned.1.call-update
  15.0 134.3 %reduce-scatter.4.cloned.1.call-done = f32[2,32,1024]{2,1,0:T(8,128)} async-done(((f32[2,1024,1024]{2,1,0:T(8,128)}), f32[2,32,1024]{2,1,0:T(8,128)}) %reduce-scatter.4.cloned.1.call-update) | async-done | bytes 262160 | tf_op jit(solution)/shard_map/reduce_scatter | solution.py:85
  149.3 1.7 bitcast_bitcast_fusion
  151.0 7.3 %all-to-all-start = ((f32[8,2,32,128]{3,2,1,0:T(8,128)}), f32[8,2,32,128]{3,2,1,0:T(8,128)S(1)}, u32[]{:S(2)}, u32[]{:S(2)}) async-start(f32[8,2,32,128]{3,2,1,0:T(8,128)} %bitcast_bitcast_fusion), calls=%async_computation.1 | async-start | bytes 524288 | tf_op jit(solution)/shard_map/all_to_all | solution.py:19
  158.3 0.0 all-gather.2.cloned.1.call-start
  158.3 0.1 compare_convert_fusion
  158.4 6.6 all-to-all-done
  165.0 0.0 copy-done.2
  165.0 0.1 multiply_add_fusion
  165.1 11.3 %all_to_all.66 = f32[8,2,32,128]{3,2,1,0:T(8,128)S(1)} all-to-all(f32[8,2,32,128]{3,2,1,0:T(8,128)S(1)} %broadcast_in_dim.22), channel_id=1, replica_groups=mesh['dp_0'=8,'dp_1'=2,'dp_2'=2,'grp'=8] {'grp'}, dimensions={0} | all-to-all | bytes 524288 | tf_op jit(solution)/shard_map/all_to_all | solution.py:25
  176.5 0.1 fusion.18
  176.6 0.1 reduce_max.18
  176.7 12.9 %all_to_all.67 = f32[32,1,2]{2,1,0:T(1,128)S(1)} all-to-all(f32[32,1,2]{2,1,0:T(1,128)S(1)} %broadcast_in_dim.23), channel_id=1, replica_groups=mesh['dp_0'=8,'dp_1'=2,'dp_2'=2,'grp'=8] {'dp_0','dp_1','dp_2'}, dimensions={0} | all-to-all | bytes 512 | tf_op jit(solution)/shard_map/all_to_all | solution.py:25
  189.6 0.1 reduce_max.19
  189.7 0.1 broadcast_multiply_fusion
  189.7 0.1 broadcast_in_dim.24
  189.9 32.2 %all_to_all.68 = f32[32,2,32,128]{3,2,1,0:T(8,128)S(1)} all-to-all(f32[32,2,32,128]{3,2,1,0:T(8,128)S(1)} %broadcast_in_dim.24), channel_id=1, replica_groups=mesh['dp_0'=8,'dp_1'=2,'dp_2'=2,'grp'=8] {'dp_0','dp_1','dp_2'}, dimensions={0} | all-to-all | bytes 2097152 | tf_op jit(solution)/shard_map/all_to_all | solution.py:25
  222.1 0.1 copy.34
  222.2 0.7 fusion.16
  222.9 11.3 %all_to_all.69 = f32[8,2,32,128]{3,2,1,0:T(8,128)S(1)} all-to-all(f32[8,2,32,128]{3,2,1,0:T(8,128)S(1)} %broadcast_in_dim.25), channel_id=1, replica_groups=mesh['dp_0'=8,'dp_1'=2,'dp_2'=2,'grp'=8] {'grp'}, dimensions={0} | all-to-all | bytes 524288 | tf_op jit(solution)/shard_map/all_to_all | solution.py:25
  234.2 0.7 convolution_subtract_fusion.3
  234.8 0.1 broadcast_in_dim.26
  235.0 31.6 %all_to_all.70 = f32[32,2,32,128]{3,2,1,0:T(8,128)S(1)} all-to-all(f32[32,2,32,128]{3,2,1,0:T(8,128)S(1)} %broadcast_in_dim.26), channel_id=1, replica_groups=mesh['dp_0'=8,'dp_1'=2,'dp_2'=2,'grp'=8] {'dp_0','dp_1','dp_2'}, dimensions={0} | all-to-all | bytes 2097152 | tf_op jit(solution)/shard_map/all_to_all | solution.py:25
  266.5 0.1 copy.36
  266.6 0.7 fusion.14
  267.3 12.2 %all_to_all.71 = f32[8,2,32,128]{3,2,1,0:T(8,128)S(1)} all-to-all(f32[8,2,32,128]{3,2,1,0:T(8,128)S(1)} %broadcast_in_dim.27), channel_id=1, replica_groups=mesh['dp_0'=8,'dp_1'=2,'dp_2'=2,'grp'=8] {'grp'}, dimensions={0} | all-to-all | bytes 524288 | tf_op jit(solution)/shard_map/all_to_all | solution.py:25
  279.6 0.7 convolution_subtract_fusion.2
  280.2 0.1 broadcast_in_dim.28
  280.4 31.6 %all_to_all.72 = f32[32,2,32,128]{3,2,1,0:T(8,128)S(1)} all-to-all(f32[32,2,32,128]{3,2,1,0:T(8,128)S(1)} %broadcast_in_dim.28), channel_id=1, replica_groups=mesh['dp_0'=8,'dp_1'=2,'dp_2'=2,'grp'=8] {'dp_0','dp_1','dp_2'}, dimensions={0} | all-to-all | bytes 2097152 | tf_op jit(solution)/shard_map/all_to_all | solution.py:25
  311.9 0.1 copy.38
  312.0 0.7 fusion.12
  312.7 12.0 %all_to_all.73 = f32[8,2,32,128]{3,2,1,0:T(8,128)S(1)} all-to-all(f32[8,2,32,128]{3,2,1,0:T(8,128)S(1)} %broadcast_in_dim.29), channel_id=1, replica_groups=mesh['dp_0'=8,'dp_1'=2,'dp_2'=2,'grp'=8] {'grp'}, dimensions={0} | all-to-all | bytes 524288 | tf_op jit(solution)/shard_map/all_to_all | solution.py:25
  324.7 0.7 convolution_subtract_fusion.1
  325.4 0.1 broadcast_in_dim.30
  325.5 31.6 %all_to_all.74 = f32[32,2,32,128]{3,2,1,0:T(8,128)S(1)} all-to-all(f32[32,2,32,128]{3,2,1,0:T(8,128)S(1)} %broadcast_in_dim.30), channel_id=1, replica_groups=mesh['dp_0'=8,'dp_1'=2,'dp_2'=2,'grp'=8] {'dp_0','dp_1','dp_2'}, dimensions={0} | all-to-all | bytes 2097152 | tf_op jit(solution)/shard_map/all_to_all | solution.py:25
  357.1 0.1 copy.40
  357.2 0.7 fusion.10
  357.9 12.1 %all_to_all.75 = f32[8,2,32,128]{3,2,1,0:T(8,128)S(1)} all-to-all(f32[8,2,32,128]{3,2,1,0:T(8,128)S(1)} %broadcast_in_dim.31), channel_id=1, replica_groups=mesh['dp_0'=8,'dp_1'=2,'dp_2'=2,'grp'=8] {'grp'}, dimensions={0} | all-to-all | bytes 524288 | tf_op jit(solution)/shard_map/all_to_all | solution.py:25
  370.0 0.7 convolution_subtract_fusion
  370.7 0.1 broadcast_in_dim.32
  370.8 31.7 %all_to_all.76 = f32[32,2,32,128]{3,2,1,0:T(8,128)S(1)} all-to-all(f32[32,2,32,128]{3,2,1,0:T(8,128)S(1)} %broadcast_in_dim.32), channel_id=1, replica_groups=mesh['dp_0'=8,'dp_1'=2,'dp_2'=2,'grp'=8] {'dp_0','dp_1','dp_2'}, dimensions={0} | all-to-all | bytes 2097152 | tf_op jit(solution)/shard_map/all_to_all | solution.py:25
  402.5 1.1 copy.42
  403.7 0.0 all-gather.2.cloned.1.call-update
  403.7 0.0 reduce-scatter.6.cloned.1.call-start
  403.7 119.5 %all-gather.2.cloned.1.call-done = f32[2,1024,1024]{2,1,0:T(8,128)} async-done(((f32[2,1024,128]{2,1,0:T(8,128)}), f32[2,1024,1024]{2,1,0:T(8,128)}) %all-gather.2.cloned.1.call-update) | async-done | bytes 8388624 | tf_op jit(solution)/shard_map/all_gather | solution.py:105
  523.3 8.6 %fusion.1 = f32[1024,512]{1,0:T(8,128)S(1)} fusion(bf16[512,1024]{1,0:T(8,128)(2,1)S(1)} %copy-done, f32[2,1024,1024]{2,1,0:T(8,128)} %all-gather.2.cloned.1.call-done), kind=kOutput, calls=%fused_computation.4 | convolution fusion | flops 6442450944 | bytes 7340032 | tf_op jit(solution)/shard_map/dot_general | solution.py:106
  531.9 0.0 copy-done.1
  531.9 8.8 %fusion = f32[1024,512]{1,0:T(8,128)S(1)} fusion(bf16[512,1024]{1,0:T(8,128)(2,1)S(1)} %copy-done.1, f32[2,1024,1024]{2,1,0:T(8,128)} %all-gather.2.cloned.1.call-done), kind=kOutput, calls=%fused_computation.2 | convolution fusion | flops 6442450944 | bytes 7340032 | tf_op jit(solution)/shard_map/dot_general | solution.py:107
  540.7 6.9 %convolution_multiply_fusion = f32[1024,1024]{1,0:T(8,128)S(1)} fusion(f32[1024,512]{1,0:T(8,128)S(1)} %fusion.1, f32[1024,512]{1,0:T(8,128)S(1)} %fusion), kind=kOutput, calls=%fused_computation.5 | convolution fusion | flops 6443499520 | bytes 8388608 | tf_op jit(solution)/shard_map/dot_general | solution.py:109
  547.6 2.2 copy.43
  549.8 0.0 reduce-scatter.6.cloned.1.call-update
  549.8 0.0 reduce-scatter.8.cloned.1.call-start
  549.9 16.7 %reduce-scatter.6.cloned.1.call-done = f32[16,32,1024]{2,1,0:T(8,128)} async-done(((f32[32,32,1024]{2,1,0:T(8,128)}), f32[16,32,1024]{2,1,0:T(8,128)}) %reduce-scatter.6.cloned.1.call-update) | async-done | bytes 2097168 | tf_op jit(solution)/shard_map/reduce_scatter | solution.py:50
  566.6 0.0 reduce-scatter.8.cloned.1.call-update
  566.6 79.0 %reduce-scatter.8.cloned.1.call-done = f32[1,32,1024]{2,1,0:T(8,128)} async-done(((f32[16,32,1024]{2,1,0:T(8,128)}), f32[1,32,1024]{2,1,0:T(8,128)}) %reduce-scatter.8.cloned.1.call-update) | async-done | bytes 131088 | tf_op jit(solution)/shard_map/reduce_scatter | solution.py:51
  645.6 0.9 copy.52
  646.5 13.2 %all_to_all.77 = f32[8,32,128]{2,1,0:T(8,128)S(1)} all-to-all(f32[8,32,128]{2,1,0:T(8,128)S(1)} %bitcast.128), channel_id=1, replica_groups=mesh['dp_0'=8,'dp_1'=2,'dp_2'=2,'grp'=8] {'grp'}, dimensions={0} | all-to-all | bytes 262144 | tf_op jit(solution)/shard_map/all_to_all | solution.py:19
  659.8 0.6 reduce_sum.29
  (13 shorter events, 0.2 us)
Async XLA Ops:
  6.5 2.9 copy-start
  6.5 142.8 %reduce-scatter.4.cloned.1.call-start = ((), (), s32[]{:S(2)}) async-start(), calls=%async_computation.16 | async-start | bytes 8650752 | tf_op jit(solution)/shard_map/reduce_scatter | solution.py:85
  15.0 150.1 %copy-start.2 = (f32[2]{0:T(128)S(1)}, f32[2]{0:T(128)}, u32[]{:S(2)}) copy-start(f32[2]{0:T(128)} %param.5) | copy-start | bytes 28
  151.0 14.0 %all-to-all-start = ((f32[8,2,32,128]{3,2,1,0:T(8,128)}), f32[8,2,32,128]{3,2,1,0:T(8,128)S(1)}, u32[]{:S(2)}, u32[]{:S(2)}) async-start(f32[8,2,32,128]{3,2,1,0:T(8,128)} %bitcast_bitcast_fusion), calls=%async_computation.1 | async-start | bytes 524288 | tf_op jit(solution)/shard_map/all_to_all | solution.py:19
  158.3 364.9 %all-gather.2.cloned.1.call-start = ((), (), s32[]{:S(2)}) async-start(), calls=%async_computation.17 | async-start | bytes 9437184 | tf_op jit(solution)/shard_map/all_gather | solution.py:105
  403.7 128.2 %copy-start.1 = (bf16[512,1024]{1,0:T(8,128)(2,1)S(1)}, bf16[512,1024]{1,0:T(8,128)(2,1)}, u32[]{:S(2)}) copy-start(bf16[512,1024]{1,0:T(8,128)(2,1)} %param.4) | copy-start | bytes 3145732
  403.7 162.9 %reduce-scatter.6.cloned.1.call-start = ((), (), s32[]{:S(2)}) async-start(), calls=%async_computation.18 | async-start | bytes 6291456 | tf_op jit(solution)/shard_map/reduce_scatter | solution.py:50
  549.8 95.8 %reduce-scatter.8.cloned.1.call-start = ((), (), s32[]{:S(2)}) async-start(), calls=%async_computation.19 | async-start | bytes 2228224 | tf_op jit(solution)/shard_map/reduce_scatter | solution.py:51
Sparse Core Ops, SparseCore 0:
  15.1 134.1 reduce-scatter.3
  403.8 119.4 all-gather.1
  549.9 16.5 reduce-scatter.5
  569.0 76.5 reduce-scatter.7
where the time goes:
time: 668 us; the launch traced here: 667 us
  waiting for transfers between devices  356 us (53%)
  blocking collectives  244 us (37%)
  matrix products  33.7 us (5%)
  between operations  13.4 us (2%)
  starting transfers between devices  7.41 us (1%)
  local copies, waits for them, and re-layouts  7.01 us (1%)
    all_to_all x11, blocking collectives, copy_for_each(): lax.all_to_all(jnp.broadcast_to(array[None], (size, *array.shape)), axis,...  231 us
    reduce_scatter x1, waiting for transfers between devices, local(): row_sums = lax.psum_scatter(stacked, DP, scatter_dimension=1, tiled=True)  134 us
    all_gather x1, waiting for transfers between devices, local(): inverses = lax.all_gather(inverse_cols, 'grp', axis=2, tiled=True)  120 us
    reduce_scatter x1, waiting for transfers between devices, summed_rows_2(): return lax.psum_scatter(pieces, chips, scatter_dimension=0, tiled=True)[0]  79 us
    reduce_scatter x1, waiting for transfers between devices, summed_rows_2(): pieces = lax.psum_scatter(pieces, core, scatter_dimension=0, tiled=True)  16.7 us
  transfers between devices with their start and end apart: 5, of which 5 were waited for; matrix products, arithmetic and copies ran while one was open for 0% of the time, Pallas kernels for 0%

commit v1 on v0

--- a/solution.py
+++ b/solution.py
@@ -102,7 +102,9 @@
         update = batched(image_rows, columns)
         iterate = 2.0 * iterate - update
     inverse_cols = collect(iterate, DP, 1)
-    inverses = lax.all_gather(inverse_cols, "grp", axis=2, tiled=True)
+    inverses = jnp.concatenate(
+        lax.all_to_all(jnp.stack([inverse_cols] * lax.axis_size("grp")), "grp", 0, 0), axis=2
+    )
     mapped = jnp.dot(acts, inverses[0], precision=highest, preferred_element_type=jnp.float32)
     weighted = jnp.dot(grads, inverses[1], precision=highest, preferred_element_type=jnp.float32)
     summed_rows = summed_rows_2(

time: 668 us -> 637 us (0.954)
  waiting for transfers between devices: 356 us -> 232 us
  blocking collectives: 244 us -> 344 us
  matrix products: 33.7 us -> 23.5 us
    all_gather x1 -> x0, waiting for transfers between devices: 120 us -> none  [local(): inverses = lax.all_gather(inverse_cols, 'grp', axis=2, tiled=True)]
    all_to_all x0 -> x1, blocking collectives: none -> 99.9 us  [local(): lax.all_to_all(jnp.stack([inverse_cols] * lax.axis_size('grp')), 'grp', 0...]
  transfers between devices with their start and end apart: 5 -> 4, of which waited for: 5 -> 4; matrix products, arithmetic and copies ran while one was open for 0% -> 0% of each run, Pallas kernels for 0% -> 0%
where the time goes in v1:
time: 637 us; the launch traced here: 636 us
  blocking collectives  344 us (54%)
  waiting for transfers between devices  232 us (36%)
  matrix products  23.5 us (4%)
  between operations  13.4 us (2%)
  local copies, waits for them, and re-layouts  10.6 us (2%)
  starting transfers between devices  7.37 us (1%)
    all_to_all x11, blocking collectives, copy_for_each(): lax.all_to_all(jnp.broadcast_to(array[None], (size, *array.shape)), axis,...  231 us
    reduce_scatter x1, waiting for transfers between devices, local(): row_sums = lax.psum_scatter(stacked, DP, scatter_dimension=1, tiled=True)  134 us
    all_to_all x1, blocking collectives, local(): lax.all_to_all(jnp.stack([inverse_cols] * lax.axis_size('grp')), 'grp', 0...  99.9 us
    reduce_scatter x1, waiting for transfers between devices, summed_rows_2(): return lax.psum_scatter(pieces, chips, scatter_dimension=0, tiled=True)[0]  79.4 us
    all_to_all x1, blocking collectives, sum_at_owner(): lax.all_to_all(pieces, axis, split_axis=0, concat_axis=0, tiled=True)  13.1 us
  transfers between devices with their start and end apart: 4, of which 4 were waited for; matrix products, arithmetic and copies ran while one was open for 0% of the time, Pallas kernels for 0%

profile of v1, /device:TPU:2, one launch (start us, length us, event | category | flops | bytes accessed | tf_op | source)
XLA Modules:
  0.0 636.4 jit_solution(12402007356754987292)
XLA Ops:
  6.5 0.0 copy-start
  6.5 0.0 reduce-scatter.4.cloned.1.call-start
  6.5 2.9 convolution_bitcast_fusion
  9.5 1.3 convolution_bitcast_fusion.1
  10.8 4.2 maximum_multiply_fusion
  15.0 0.0 reduce-scatter.4.cloned.1.call-update
  15.0 134.3 %reduce-scatter.4.cloned.1.call-done = f32[2,32,1024]{2,1,0:T(8,128)} async-done(((f32[2,1024,1024]{2,1,0:T(8,128)}), f32[2,32,1024]{2,1,0:T(8,128)}) %reduce-scatter.4.cloned.1.call-update) | async-done | bytes 262160 | tf_op jit(solution)/shard_map/reduce_scatter | solution.py:85
  149.3 1.7 bitcast_bitcast_fusion
  151.0 7.3 %all-to-all-start = ((f32[8,2,32,128]{3,2,1,0:T(8,128)}), f32[8,2,32,128]{3,2,1,0:T(8,128)S(1)}, u32[]{:S(2)}, u32[]{:S(2)}) async-start(f32[8,2,32,128]{3,2,1,0:T(8,128)} %bitcast_bitcast_fusion), calls=%async_computation.1 | async-start | bytes 524288 | tf_op jit(solution)/shard_map/all_to_all | solution.py:19
  158.3 0.1 compare_convert_fusion
  158.4 6.6 %all-to-all-done = f32[8,2,32,128]{3,2,1,0:T(8,128)S(1)} async-done(((f32[8,2,32,128]{3,2,1,0:T(8,128)}), f32[8,2,32,128]{3,2,1,0:T(8,128)S(1)}, u32[]{:S(2)}, u32[]{:S(2)}) %all-to-all-start) | async-done | bytes 262176 | tf_op jit(solution)/shard_map/all_to_all | solution.py:19
  165.0 0.0 copy-done.2
  165.0 0.1 multiply_add_fusion
  165.1 11.3 %all_to_all.71 = f32[8,2,32,128]{3,2,1,0:T(8,128)S(1)} all-to-all(f32[8,2,32,128]{3,2,1,0:T(8,128)S(1)} %broadcast_in_dim.22), channel_id=1, replica_groups=mesh['dp_0'=8,'dp_1'=2,'dp_2'=2,'grp'=8] {'grp'}, dimensions={0} | all-to-all | bytes 524288 | tf_op jit(solution)/shard_map/all_to_all | solution.py:25
  176.5 0.1 fusion.16
  176.6 0.1 reduce_max.18
  176.7 12.9 %all_to_all.72 = f32[32,1,2]{2,1,0:T(1,128)S(1)} all-to-all(f32[32,1,2]{2,1,0:T(1,128)S(1)} %broadcast_in_dim.23), channel_id=1, replica_groups=mesh['dp_0'=8,'dp_1'=2,'dp_2'=2,'grp'=8] {'dp_0','dp_1','dp_2'}, dimensions={0} | all-to-all | bytes 512 | tf_op jit(solution)/shard_map/all_to_all | solution.py:25
  189.6 0.1 reduce_max.19
  189.7 0.1 broadcast_multiply_fusion
  189.7 0.1 broadcast_in_dim.24
  189.9 32.2 %all_to_all.73 = f32[32,2,32,128]{3,2,1,0:T(8,128)S(1)} all-to-all(f32[32,2,32,128]{3,2,1,0:T(8,128)S(1)} %broadcast_in_dim.24), channel_id=1, replica_groups=mesh['dp_0'=8,'dp_1'=2,'dp_2'=2,'grp'=8] {'dp_0','dp_1','dp_2'}, dimensions={0} | all-to-all | bytes 2097152 | tf_op jit(solution)/shard_map/all_to_all | solution.py:25
  222.1 0.1 copy.39
  222.2 0.7 fusion.14
  222.9 11.3 %all_to_all.74 = f32[8,2,32,128]{3,2,1,0:T(8,128)S(1)} all-to-all(f32[8,2,32,128]{3,2,1,0:T(8,128)S(1)} %broadcast_in_dim.25), channel_id=1, replica_groups=mesh['dp_0'=8,'dp_1'=2,'dp_2'=2,'grp'=8] {'grp'}, dimensions={0} | all-to-all | bytes 524288 | tf_op jit(solution)/shard_map/all_to_all | solution.py:25
  234.2 0.7 convolution_subtract_fusion.3
  234.8 0.1 broadcast_in_dim.26
  235.0 31.6 %all_to_all.75 = f32[32,2,32,128]{3,2,1,0:T(8,128)S(1)} all-to-all(f32[32,2,32,128]{3,2,1,0:T(8,128)S(1)} %broadcast_in_dim.26), channel_id=1, replica_groups=mesh['dp_0'=8,'dp_1'=2,'dp_2'=2,'grp'=8] {'dp_0','dp_1','dp_2'}, dimensions={0} | all-to-all | bytes 2097152 | tf_op jit(solution)/shard_map/all_to_all | solution.py:25
  266.5 0.1 copy.41
  266.6 0.7 fusion.12
  267.3 12.2 %all_to_all.76 = f32[8,2,32,128]{3,2,1,0:T(8,128)S(1)} all-to-all(f32[8,2,32,128]{3,2,1,0:T(8,128)S(1)} %broadcast_in_dim.27), channel_id=1, replica_groups=mesh['dp_0'=8,'dp_1'=2,'dp_2'=2,'grp'=8] {'grp'}, dimensions={0} | all-to-all | bytes 524288 | tf_op jit(solution)/shard_map/all_to_all | solution.py:25
  279.6 0.7 convolution_subtract_fusion.2
  280.2 0.1 broadcast_in_dim.28
  280.4 31.6 %all_to_all.77 = f32[32,2,32,128]{3,2,1,0:T(8,128)S(1)} all-to-all(f32[32,2,32,128]{3,2,1,0:T(8,128)S(1)} %broadcast_in_dim.28), channel_id=1, replica_groups=mesh['dp_0'=8,'dp_1'=2,'dp_2'=2,'grp'=8] {'dp_0','dp_1','dp_2'}, dimensions={0} | all-to-all | bytes 2097152 | tf_op jit(solution)/shard_map/all_to_all | solution.py:25
  311.9 0.1 copy.43
  312.0 0.7 fusion.10
  312.7 12.0 %all_to_all.78 = f32[8,2,32,128]{3,2,1,0:T(8,128)S(1)} all-to-all(f32[8,2,32,128]{3,2,1,0:T(8,128)S(1)} %broadcast_in_dim.29), channel_id=1, replica_groups=mesh['dp_0'=8,'dp_1'=2,'dp_2'=2,'grp'=8] {'grp'}, dimensions={0} | all-to-all | bytes 524288 | tf_op jit(solution)/shard_map/all_to_all | solution.py:25
  324.7 0.7 convolution_subtract_fusion.1
  325.4 0.1 broadcast_in_dim.30
  325.5 31.6 %all_to_all.79 = f32[32,2,32,128]{3,2,1,0:T(8,128)S(1)} all-to-all(f32[32,2,32,128]{3,2,1,0:T(8,128)S(1)} %broadcast_in_dim.30), channel_id=1, replica_groups=mesh['dp_0'=8,'dp_1'=2,'dp_2'=2,'grp'=8] {'dp_0','dp_1','dp_2'}, dimensions={0} | all-to-all | bytes 2097152 | tf_op jit(solution)/shard_map/all_to_all | solution.py:25
  357.1 0.1 copy.45
  357.2 0.7 fusion.8
  357.9 12.1 %all_to_all.80 = f32[8,2,32,128]{3,2,1,0:T(8,128)S(1)} all-to-all(f32[8,2,32,128]{3,2,1,0:T(8,128)S(1)} %broadcast_in_dim.31), channel_id=1, replica_groups=mesh['dp_0'=8,'dp_1'=2,'dp_2'=2,'grp'=8] {'grp'}, dimensions={0} | all-to-all | bytes 524288 | tf_op jit(solution)/shard_map/all_to_all | solution.py:25
  370.0 0.7 convolution_subtract_fusion
  370.7 0.1 broadcast_in_dim.32
  370.8 31.7 %all_to_all.81 = f32[32,2,32,128]{3,2,1,0:T(8,128)S(1)} all-to-all(f32[32,2,32,128]{3,2,1,0:T(8,128)S(1)} %broadcast_in_dim.32), channel_id=1, replica_groups=mesh['dp_0'=8,'dp_1'=2,'dp_2'=2,'grp'=8] {'dp_0','dp_1','dp_2'}, dimensions={0} | all-to-all | bytes 2097152 | tf_op jit(solution)/shard_map/all_to_all | solution.py:25
  402.5 0.1 copy.47
  402.6 0.3 copy.48
  402.9 1.1 stack.15
  404.0 99.9 %all_to_all.82 = f32[8,2,1024,128]{2,3,1,0:T(8,128)S(1)} all-to-all(f32[8,2,1024,128]{2,3,1,0:T(8,128)S(1)} %stack.15), channel_id=1, replica_groups=mesh['dp_0'=8,'dp_1'=2,'dp_2'=2,'grp'=8] {'grp'}, dimensions={0} | all-to-all | bytes 16777216 | tf_op jit(solution)/shard_map/all_to_all | solution.py:106
  503.9 1.7 copy.95
  505.6 1.7 fusion.21
  507.2 0.0 copy-start.1
  507.2 3.5 fusion.22
  510.8 3.5 fusion.23
  514.2 7.1 %convolution_multiply_fusion = f32[1024,1024]{1,0:T(8,128)S(1)} fusion(f32[1024,512]{1,0:T(8,128)S(1)} %fusion.22, f32[1024,512]{1,0:T(8,128)S(1)} %fusion.23), kind=kOutput, calls=%fused_computation.2 | convolution fusion | flops 6443499520 | bytes 8388608 | tf_op jit(solution)/shard_map/dot_general | solution.py:111
  521.4 2.2 copy.50
  523.6 0.0 reduce-scatter.6.cloned.1.call-update
  523.6 0.0 reduce-scatter.8.cloned.1.call-start
  523.7 12.1 %reduce-scatter.6.cloned.1.call-done = f32[16,32,1024]{2,1,0:T(8,128)} async-done(((f32[32,32,1024]{2,1,0:T(8,128)}), f32[16,32,1024]{2,1,0:T(8,128)}) %reduce-scatter.6.cloned.1.call-update) | async-done | bytes 2097168 | tf_op jit(solution)/shard_map/reduce_scatter | solution.py:50
  535.8 0.0 reduce-scatter.8.cloned.1.call-update
  535.8 79.4 %reduce-scatter.8.cloned.1.call-done = f32[1,32,1024]{2,1,0:T(8,128)} async-done(((f32[16,32,1024]{2,1,0:T(8,128)}), f32[1,32,1024]{2,1,0:T(8,128)}) %reduce-scatter.8.cloned.1.call-update) | async-done | bytes 131088 | tf_op jit(solution)/shard_map/reduce_scatter | solution.py:51
  615.2 0.9 copy.59
  616.2 13.1 %all_to_all.83 = f32[8,32,128]{2,1,0:T(8,128)S(1)} all-to-all(f32[8,32,128]{2,1,0:T(8,128)S(1)} %bitcast.132), channel_id=1, replica_groups=mesh['dp_0'=8,'dp_1'=2,'dp_2'=2,'grp'=8] {'grp'}, dimensions={0} | all-to-all | bytes 262144 | tf_op jit(solution)/shard_map/all_to_all | solution.py:19
  629.2 0.6 reduce_sum.29
  (15 shorter events, 0.2 us)
Async XLA Ops:
  6.5 2.9 copy-start
  6.5 142.8 %reduce-scatter.4.cloned.1.call-start = ((), (), s32[]{:S(2)}) async-start(), calls=%async_computation.17 | async-start | bytes 8650752 | tf_op jit(solution)/shard_map/reduce_scatter | solution.py:85
  15.0 150.1 %copy-start.2 = (f32[2]{0:T(128)S(1)}, f32[2]{0:T(128)}, u32[]{:S(2)}) copy-start(f32[2]{0:T(128)} %param.5) | copy-start | bytes 28
  151.0 14.0 %all-to-all-start = ((f32[8,2,32,128]{3,2,1,0:T(8,128)}), f32[8,2,32,128]{3,2,1,0:T(8,128)S(1)}, u32[]{:S(2)}, u32[]{:S(2)}) async-start(f32[8,2,32,128]{3,2,1,0:T(8,128)} %bitcast_bitcast_fusion), calls=%async_computation.1 | async-start | bytes 524288 | tf_op jit(solution)/shard_map/all_to_all | solution.py:19
  158.3 377.5 %reduce-scatter.6.cloned.1.call-start = ((), (), s32[]{:S(2)}) async-start(), calls=%async_computation.18 | async-start | bytes 6291456 | tf_op jit(solution)/shard_map/reduce_scatter | solution.py:50
  507.2 3.5 copy-start.1
  523.6 91.6 %reduce-scatter.8.cloned.1.call-start = ((), (), s32[]{:S(2)}) async-start(), calls=%async_computation.19 | async-start | bytes 2228224 | tf_op jit(solution)/shard_map/reduce_scatter | solution.py:51
Sparse Core Ops, SparseCore 0:
  15.1 134.1 reduce-scatter.3
  523.7 12.0 reduce-scatter.5
  538.3 76.8 reduce-scatter.7
